TPU v7x, 32 devices: a whole 2x2x4 slice. The times are simulated.
32 devices in a mesh: row: 8 (over z, x), col: 4 (over y, core).
Axes of the slice: x: 2, y: 2, z: 4, core: 2. Of those that a mesh axis runs over, the one named last changes fastest.
Arguments:
- tokens: bfloat16 [64, 12288], P('row', 'col'), may hold values from -6 to 6
- past_tokens: bfloat16 [64, 12288], P('row', 'col'), may hold values from -6 to 6
- out_grad: bfloat16 [64, 12288], P('row', 'col'), may hold values from -3 to 3
- w_in: bfloat16 [12288, 24576], P('col', 'row'), may hold values from -0.0546875 to 0.0546875
- w_out: bfloat16 [24576, 12288], P('row', 'col'), may hold values from -0.0390625 to 0.0390625
Outputs:
- layer_out: bfloat16 [64, 12288], P('row', 'col')
- input_grad: bfloat16 [64, 12288], P('row', 'col')
- grad_w_in: bfloat16 [12288, 24576], P('col', 'row')
- grad_w_out: bfloat16 [24576, 12288], P('row', 'col')
All inputs are finite; a program needn't handle non-finite values.
Results may differ from a plain program's by a relative error of at most 0.005.
Values may be sent and summed in bfloat16 or wider, within the bound.
No kernel may reach another device: no remote copies, remote signals or barrier semaphores. Data moves between devices by JAX's collectives and lax.ppermute only.
A program may use at most 128 MiB of HBM per device.

v0:
```python
import jax
import jax.numpy as jnp
from jax import lax
from jax.sharding import PartitionSpec as P


def gelu_parts(pre):
    cdf = 0.5 * (1.0 + jax.scipy.special.erf(pre * 0.7071067811865476))
    slope = cdf + pre * jnp.exp(-0.5 * pre * pre) * 0.3989422804014327
    return (pre * cdf, slope)


def local(tokens, past_tokens, out_grad, w_in, w_out):
    pre_part = jnp.dot(
        lax.all_gather(tokens, "row", axis=0, tiled=True), w_in, preferred_element_type=jnp.float32
    )
    pre_share = lax.psum_scatter(pre_part, "col", scatter_dimension=0, tiled=True)
    hidden_share = gelu_parts(pre_share)[0].astype(jnp.bfloat16)
    hidden_all = lax.all_gather(hidden_share, "col", axis=0, tiled=True)
    block = hidden_all
    layer_out = lax.psum_scatter(
        jnp.dot(block, w_out, preferred_element_type=jnp.float32),
        "row",
        scatter_dimension=0,
        tiled=True,
    ).astype(jnp.bfloat16)
    past_all, grad_all = (
        lax.all_gather(past_tokens, "row", axis=0, tiled=True),
        lax.all_gather(out_grad, "row", axis=0, tiled=True),
    )
    past_part = jnp.dot(past_all, w_in, preferred_element_type=jnp.float32)
    back_part = lax.dot_general(
        grad_all, w_out, (((1,), (1,)), ((), ())), preferred_element_type=jnp.float32
    )
    past_share, back_share = (
        lax.psum_scatter(past_part, "col", scatter_dimension=0, tiled=True),
        lax.psum_scatter(back_part, "col", scatter_dimension=0, tiled=True),
    )
    act_share, slope = gelu_parts(past_share)
    act_local = act_share.astype(jnp.bfloat16)
    grad_local = (back_share * slope).astype(jnp.bfloat16)
    act_all, hidden_grad = (
        lax.all_gather(act_local, "col", axis=0, tiled=True),
        lax.all_gather(grad_local, "col", axis=0, tiled=True),
    )
    grad_w_out = lax.dot_general(
        act_all, grad_all, (((0,), (0,)), ((), ())), preferred_element_type=jnp.float32
    ).astype(jnp.bfloat16)
    grad_w_in = lax.dot_general(
        past_all, hidden_grad, (((0,), (0,)), ((), ())), preferred_element_type=jnp.float32
    ).astype(jnp.bfloat16)
    block = hidden_grad
    input_grad = lax.psum_scatter(
        lax.dot_general(block, w_in, (((1,), (1,)), ((), ())), preferred_element_type=jnp.float32),
        "row",
        scatter_dimension=0,
        tiled=True,
    ).astype(jnp.bfloat16)
    return (layer_out, input_grad, grad_w_in, grad_w_out)


def solution(mesh):
    in_specs = (P("row", "col"), P("row", "col"), P("row", "col"), P("col", "row"), P("row", "col"))
    out_specs = (P("row", "col"), P("row", "col"), P("col", "row"), P("row", "col"))
    return jax.shard_map(local, mesh=mesh, in_specs=in_specs, out_specs=out_specs, check_vma=False)
```

profile of v0, /device:TPU:0, one launch (start us, length us, event | category | flops | bytes accessed | tf_op | source)
XLA Modules:
  0.0 301.0 jit_solution(17160969050519650466)
XLA Ops:
  7.2 0.0 reduce-scatter.6.cloned.1.call-start
  7.2 33.0 %all_gather.18 = bf16[64,3072]{1,0:T(8,128)(2,1)S(1)} all-gather(bf16[8,3072]{1,0:T(8,128)(2,1)} %param.5), channel_id=1, replica_groups=mesh['row'=8,'col'=4] {'row'}, dimensions={0}, use_global_device_ids=true | all-gather | bytes 442368 | tf_op jit(solution)/shard_map/all_gather | solution.py:15
  40.2 10.6 %fusion.6 = f32[64,3072]{1,0:T(8,128)} fusion(bf16[64,3072]{1,0:T(8,128)(2,1)S(1)} %all_gather.18, bf16[3072,3072]{1,0:T(8,128)(2,1)} %param.8), kind=kOutput, calls=%fused_computation.12 | convolution fusion | flops 1207959552 | bytes 20054016 | tf_op jit(solution)/shard_map/dot_general | solution.py:14
  50.8 0.0 reduce-scatter.6.cloned.1.call-update
  50.9 0.0 reduce-scatter.10.cloned.1.call-start
  50.9 31.0 %all_gather.20 = bf16[64,3072]{1,0:T(8,128)(2,1)S(1)} all-gather(bf16[8,3072]{1,0:T(8,128)(2,1)S(1)} %copy-done), channel_id=1, replica_groups=mesh['row'=8,'col'=4] {'row'}, dimensions={0}, use_global_device_ids=true | all-gather | bytes 442368 | tf_op jit(solution)/shard_map/all_gather | solution.py:29
  81.9 13.1 %fusion.8 = f32[64,3072]{1,0:T(8,128)} fusion(bf16[64,3072]{1,0:T(8,128)(2,1)S(1)} %all_gather.20, bf16[3072,3072]{1,0:T(8,128)(2,1)} %param.9), kind=kOutput, calls=%fused_computation.14 | convolution fusion | flops 1207959552 | bytes 20054016 | tf_op jit(solution)/shard_map/dot_general | solution.py:32
  95.0 0.0 reduce-scatter.10.cloned.1.call-update
  95.0 0.0 reduce-scatter.12.cloned.1.call-start
  95.0 31.0 %all_gather.21 = bf16[64,3072]{1,0:T(8,128)(2,1)S(1)} all-gather(bf16[8,3072]{1,0:T(8,128)(2,1)S(1)} %copy-done.1), channel_id=1, replica_groups=mesh['row'=8,'col'=4] {'row'}, dimensions={0}, use_global_device_ids=true | all-gather | bytes 442368 | tf_op jit(solution)/shard_map/all_gather | solution.py:28
  126.0 10.6 %fusion.9 = f32[64,3072]{1,0:T(8,128)} fusion(bf16[64,3072]{1,0:T(8,128)(2,1)S(1)} %all_gather.21, bf16[3072,3072]{1,0:T(8,128)(2,1)} %param.8), kind=kOutput, calls=%fused_computation.15 | convolution fusion | flops 1207959552 | bytes 20054016 | tf_op jit(solution)/shard_map/dot_general | solution.py:31
  136.6 0.0 reduce-scatter.12.cloned.1.call-update
  136.7 0.0 reduce-scatter.8.cloned.1.call-start
  136.7 0.0 reduce-scatter.6.cloned.1.call-done
  136.7 1.0 multiply_convert_fusion.1
  137.7 6.7 %all_gather.19 = bf16[64,3072]{1,0:T(8,128)(2,1)S(1)} all-gather(bf16[16,3072]{1,0:T(8,128)(2,1)S(1)} %multiply_convert_fusion.1), channel_id=1, replica_groups=mesh['row'=8,'col'=4] {'col'}, dimensions={0}, use_global_device_ids=true | all-gather | bytes 491520 | tf_op jit(solution)/shard_map/all_gather | solution.py:19
  144.4 10.8 %fusion.7 = f32[64,3072]{1,0:T(8,128)} fusion(bf16[64,3072]{1,0:T(8,128)(2,1)S(1)} %all_gather.19, bf16[3072,3072]{1,0:T(8,128)(2,1)} %param.9), kind=kOutput, calls=%fused_computation.13 | convolution fusion | flops 1207959552 | bytes 20054016 | tf_op jit(solution)/shard_map/dot_general | solution.py:22
  155.2 0.0 reduce-scatter.8.cloned.1.call-update
  155.2 0.0 reduce-scatter.14.cloned.1.call-start
  155.3 0.0 reduce-scatter.10.cloned.1.call-done
  155.3 5.8 %reduce-scatter.12.cloned.1.call-done = f32[16,3072]{1,0:T(8,128)} async-done(((f32[64,3072]{1,0:T(8,128)}), f32[16,3072]{1,0:T(8,128)}) %reduce-scatter.12.cloned.1.call-update) | async-done | bytes 196624 | tf_op jit(solution)/shard_map/reduce_scatter | solution.py:36
  161.1 1.1 multiply_convert_fusion
  162.2 6.1 %all_gather.22 = bf16[64,3072]{1,0:T(8,128)(2,1)S(1)} all-gather(bf16[16,3072]{1,0:T(8,128)(2,1)S(1)} %get-tuple-element.9), channel_id=1, replica_groups=mesh['row'=8,'col'=4] {'col'}, dimensions={0}, use_global_device_ids=true | all-gather | bytes 491520 | tf_op jit(solution)/shard_map/all_gather | solution.py:44
  168.3 13.1 %fusion.10 = f32[64,3072]{1,0:T(8,128)} fusion(bf16[64,3072]{1,0:T(8,128)(2,1)S(1)} %all_gather.22, bf16[3072,3072]{1,0:T(8,128)(2,1)} %param.8), kind=kOutput, calls=%fused_computation.16 | convolution fusion | flops 1207959552 | bytes 20054016 | tf_op jit(solution)/shard_map/dot_general | solution.py:54
  181.5 0.0 reduce-scatter.14.cloned.1.call-update
  181.5 9.5 %convert_bitcast_fusion = bf16[3072,3072]{0,1:T(8,128)(2,1)} fusion(bf16[64,3072]{1,0:T(8,128)(2,1)S(1)} %all_gather.22, bf16[64,3072]{1,0:T(8,128)(2,1)S(1)} %all_gather.21), kind=kOutput, calls=%fused_computation | convolution fusion | flops 1217396736 | bytes 19660800 | tf_op jit(solution)/shard_map/dot_general | solution.py:49
  191.0 24.6 %copy.9 = bf16[3072,3072]{1,0:T(8,128)(2,1)} copy(bf16[3072,3072]{0,1:T(8,128)(2,1)} %convert_bitcast_fusion) | data formatting | bytes 37748736
  215.6 6.7 %all_gather.23 = bf16[64,3072]{1,0:T(8,128)(2,1)S(1)} all-gather(bf16[16,3072]{1,0:T(8,128)(2,1)S(1)} %get-tuple-element.8), channel_id=1, replica_groups=mesh['row'=8,'col'=4] {'col'}, dimensions={0}, use_global_device_ids=true | all-gather | bytes 491520 | tf_op jit(solution)/shard_map/all_gather | solution.py:43
  222.4 9.5 %convolution_convert_fusion = bf16[3072,3072]{1,0:T(8,128)(2,1)} fusion(bf16[64,3072]{1,0:T(8,128)(2,1)S(1)} %all_gather.23, bf16[64,3072]{1,0:T(8,128)(2,1)S(1)} %all_gather.20), kind=kOutput, calls=%fused_computation.1 | convolution fusion | flops 1217396736 | bytes 19660800 | tf_op jit(solution)/shard_map/dot_general | solution.py:46
  231.9 1.5 convert_element_type.25
  233.4 59.5 %reduce-scatter.14.cloned.1.call-done = f32[8,3072]{1,0:T(8,128)} async-done(((f32[64,3072]{1,0:T(8,128)}), f32[8,3072]{1,0:T(8,128)}) %reduce-scatter.14.cloned.1.call-update) | async-done | bytes 98320 | tf_op jit(solution)/shard_map/reduce_scatter | solution.py:53
  292.9 1.5 convert_element_type.27
  (5 shorter events, 0.0 us)
Async XLA Ops:
  7.2 43.8 %copy-start = (bf16[8,3072]{1,0:T(8,128)(2,1)S(1)}, bf16[8,3072]{1,0:T(8,128)(2,1)}, u32[]{:S(2)}) copy-start(bf16[8,3072]{1,0:T(8,128)(2,1)} %param.7) | copy-start | bytes 147460
  7.2 129.6 %reduce-scatter.6.cloned.1.call-start = ((), (), s32[]{:S(2)}) async-start(), calls=%async_computation.5 | async-start | bytes 983040 | tf_op jit(solution)/shard_map/reduce_scatter | solution.py:17
  40.2 54.8 %copy-start.1 = (bf16[8,3072]{1,0:T(8,128)(2,1)S(1)}, bf16[8,3072]{1,0:T(8,128)(2,1)}, u32[]{:S(2)}) copy-start(bf16[8,3072]{1,0:T(8,128)(2,1)} %param.6) | copy-start | bytes 147460
  50.9 104.4 %reduce-scatter.10.cloned.1.call-start = ((), (), s32[]{:S(2)}) async-start(), calls=%async_computation.7 | async-start | bytes 983040 | tf_op jit(solution)/shard_map/reduce_scatter | solution.py:37
  95.0 66.1 %reduce-scatter.12.cloned.1.call-start = ((), (), s32[]{:S(2)}) async-start(), calls=%async_computation.8 | async-start | bytes 983040 | tf_op jit(solution)/shard_map/reduce_scatter | solution.py:36
  136.7 95.2 %reduce-scatter.8.cloned.1.call-start = ((), (), s32[]{:S(2)}) async-start(), calls=%async_computation.6 | async-start | bytes 884736 | tf_op jit(solution)/shard_map/reduce_scatter | solution.py:21
  155.2 137.7 %reduce-scatter.14.cloned.1.call-start = ((), (), s32[]{:S(2)}) async-start(), calls=%async_computation.9 | async-start | bytes 884736 | tf_op jit(solution)/shard_map/reduce_scatter | solution.py:53
Sparse Core Ops, SparseCore 0:
  51.0 24.2 reduce-scatter.5
  95.1 24.2 reduce-scatter.9
  136.8 24.2 reduce-scatter.11
  164.2 63.2 reduce-scatter.7
  230.6 62.2 reduce-scatter.13
where the time goes:
time: 302 us; the launch traced here: 301 us
  blocking collectives  114 us (38%)
  matrix products  77.3 us (26%)
  waiting for transfers between devices  65.4 us (22%)
  local copies, waits for them, and re-layouts  24.6 us (8%)
  between operations  13.8 us (5%)
  other arithmetic  5.13 us (2%)
    reduce_scatter x1, waiting for transfers between devices, local(): lax.psum_scatter(lax.dot_general(block, w_in, (((1,), (1,)), ((), ())), p...  59.5 us
    all_gather x1, blocking collectives, local(): lax.all_gather(tokens, 'row', axis=0, tiled=True)  33 us
    all_gather x1, blocking collectives, local(): lax.all_gather(out_grad, 'row', axis=0, tiled=True)  31 us
    all_gather x1, blocking collectives, local(): lax.all_gather(past_tokens, 'row', axis=0, tiled=True)  31 us
    unnamed x5, local copies, waits for them, and re-layouts  24.6 us
    dot_general x1, matrix products, local(): lax.dot_general(block, w_in, (((1,), (1,)), ((), ())), preferred_element_...  13.1 us
    dot_general x1, matrix products, local(): lax.dot_general(grad_all, w_out, (((1,), (1,)), ((), ())), preferred_elem...  13.1 us
    dot_general x1, matrix products, local(): jnp.dot(block, w_out, preferred_element_type=jnp.float32)  10.8 us
  transfers between devices with their start and end apart: 5, of which 2 were waited for; matrix products, arithmetic and copies ran while one was open for 32% of the time, Pallas kernels for 0%

commit v1 on v0

--- a/solution.py
+++ b/solution.py
@@ -2,6 +2,27 @@
 import jax.numpy as jnp
 from jax import lax
 from jax.sharding import PartitionSpec as P
+
+
+def ring_gather(x, axis, dim):
+    size, index, rows = (lax.axis_size(axis), lax.axis_index(axis), x.shape[dim])
+    right = [(i, (i + 1) % size) for i in range(size)]
+    left = [(i, (i - 1) % size) for i in range(size)]
+    result = jnp.zeros((*x.shape[:dim], size * rows, *x.shape[dim + 1 :]), x.dtype)
+    result = lax.dynamic_update_slice_in_dim(result, x, index * rows, axis=dim)
+    from_left = from_right = x
+    half = size // 2
+    for step in range(1, half + 1):
+        from_left = lax.ppermute(from_left, axis, right)
+        result = lax.dynamic_update_slice_in_dim(
+            result, from_left, (index - step) % size * rows, axis=dim
+        )
+        if step < size - half:
+            from_right = lax.ppermute(from_right, axis, left)
+            result = lax.dynamic_update_slice_in_dim(
+                result, from_right, (index + step) % size * rows, axis=dim
+            )
+    return result
 
 
 def gelu_parts(pre):
@@ -11,9 +32,7 @@
 
 
 def local(tokens, past_tokens, out_grad, w_in, w_out):
-    pre_part = jnp.dot(
-        lax.all_gather(tokens, "row", axis=0, tiled=True), w_in, preferred_element_type=jnp.float32
-    )
+    pre_part = jnp.dot(ring_gather(tokens, "row", 0), w_in, preferred_element_type=jnp.float32)
     pre_share = lax.psum_scatter(pre_part, "col", scatter_dimension=0, tiled=True)
     hidden_share = gelu_parts(pre_share)[0].astype(jnp.bfloat16)
     hidden_all = lax.all_gather(hidden_share, "col", axis=0, tiled=True)

time: 302 us -> 297 us (0.983)
  blocking collectives: 114 us -> 83.9 us
  starting transfers between devices: 0.21 us -> 14.4 us
  waiting for transfers between devices: 65.4 us -> 76.6 us
    reduce_scatter x1, waiting for transfers between devices: 0.01 us -> 61.2 us  [local(): lax.psum_scatter(jnp.dot(block, w_out, preferred_element_type=jnp.float32...]
    reduce_scatter x1, waiting for transfers between devices: 59.5 us -> 0.01 us  [local(): lax.psum_scatter(lax.dot_general(block, w_in, (((1,), (1,)), ((), ())), p...]
    all_gather x1 -> x0, blocking collectives: 33 us -> none  [local(): lax.all_gather(tokens, 'row', axis=0, tiled=True)]
    ppermute x0 -> x7, waiting for transfers between devices: none -> 15.2 us  [the longest x4 13.5 us: ring_gather(): from_left = lax.ppermute(from_left, axis, right)]
    ppermute x0 -> x7, starting transfers between devices: none -> 14.2 us  [the longest x3 14.2 us: ring_gather(): from_right = lax.ppermute(from_right, axis, left)]
    reduce_scatter x1, waiting for transfers between devices: 5.76 us -> 0.02 us  [local(): lax.psum_scatter(past_part, 'col', scatter_dimension=0, tiled=True)]
  transfers between devices with their start and end apart: 5 -> 12, of which waited for: 2 -> 4; matrix products, arithmetic and copies ran while one was open for 32% -> 31% of each run, Pallas kernels for 0% -> 0%
where the time goes in v1:
time: 297 us; the launch traced here: 296 us
  blocking collectives  83.9 us (28%)
  matrix products  77.3 us (26%)
  waiting for transfers between devices  76.6 us (26%)
  local copies, waits for them, and re-layouts  24.7 us (8%)
  starting transfers between devices  14.4 us (5%)
  between operations  14 us (5%)
  other arithmetic  5.13 us (2%)
    reduce_scatter x1, waiting for transfers between devices, local(): lax.psum_scatter(jnp.dot(block, w_out, preferred_element_type=jnp.float32...  61.2 us
    all_gather x1, blocking collectives, local(): lax.all_gather(out_grad, 'row', axis=0, tiled=True)  33 us
    all_gather x1, blocking collectives, local(): lax.all_gather(past_tokens, 'row', axis=0, tiled=True)  31 us
    unnamed x5, local copies, waits for them, and re-layouts  24.6 us
    ppermute x3, starting transfers between devices, ring_gather(): from_right = lax.ppermute(from_right, axis, left)  14.2 us
    ppermute x4, waiting for transfers between devices, ring_gather(): from_left = lax.ppermute(from_left, axis, right)  13.5 us
    dot_general x1, matrix products, local(): lax.dot_general(block, w_in, (((1,), (1,)), ((), ())), preferred_element_...  13.2 us
    dot_general x1, matrix products, local(): lax.dot_general(grad_all, w_out, (((1,), (1,)), ((), ())), preferred_elem...  13.1 us
  transfers between devices with their start and end apart: 12, of which 4 were waited for; matrix products, arithmetic and copies ran while one was open for 31% of the time, Pallas kernels for 0%

profile of v1, /device:TPU:0, one launch (start us, length us, event | category | flops | bytes accessed | tf_op | source)
XLA Modules:
  0.0 296.1 jit_solution(5172029676531698970)
XLA Ops:
  7.2 0.0 reduce-scatter.10.cloned.1.call-start
  7.2 33.0 %all_gather.16 = bf16[64,3072]{1,0:T(8,128)(2,1)S(1)} all-gather(bf16[8,3072]{1,0:T(8,128)(2,1)} %param.7), channel_id=1, replica_groups=mesh['row'=8,'col'=4] {'row'}, dimensions={0}, use_global_device_ids=true | all-gather | bytes 442368 | tf_op jit(solution)/shard_map/all_gather | solution.py:48
  40.2 13.1 %fusion.8 = f32[64,3072]{1,0:T(8,128)} fusion(bf16[64,3072]{1,0:T(8,128)(2,1)S(1)} %all_gather.16, bf16[3072,3072]{1,0:T(8,128)(2,1)} %param.9), kind=kOutput, calls=%fused_computation.22 | convolution fusion | flops 1207959552 | bytes 20054016 | tf_op jit(solution)/shard_map/dot_general | solution.py:51
  53.3 0.0 reduce-scatter.12.cloned.1.call-start
  53.4 4.4 %collective-permute-start.1 = (bf16[8,3072]{1,0:T(8,128)(2,1)S(1)}, bf16[8,3072]{1,0:T(8,128)(2,1)S(1)}, u32[]{:S(2)}, u32[]{:S(2)}) collective-permute-start(bf16[8,3072]{1,0:T(8,128)(2,1)S(1)} %copy-done.1), channel_id=1, source_target_pairs={{0,28},{4,0},{8,4},{12,8},{16,12},{20,16},{24,20},{28,24},{1,29},{... | collective-permute-start | bytes 147464 | tf_op jit(solution)/shard_map/ppermute | solution.py:21
  57.7 31.0 %all_gather.17 = bf16[64,3072]{1,0:T(8,128)(2,1)S(1)} all-gather(bf16[8,3072]{1,0:T(8,128)(2,1)S(1)} %copy-done), channel_id=1, replica_groups=mesh['row'=8,'col'=4] {'row'}, dimensions={0}, use_global_device_ids=true | all-gather | bytes 442368 | tf_op jit(solution)/shard_map/all_gather | solution.py:47
  88.7 10.6 %fusion.9 = f32[64,3072]{1,0:T(8,128)} fusion(bf16[64,3072]{1,0:T(8,128)(2,1)S(1)} %all_gather.17, bf16[3072,3072]{1,0:T(8,128)(2,1)} %param.8), kind=kOutput, calls=%fused_computation.23 | convolution fusion | flops 1207959552 | bytes 20054016 | tf_op jit(solution)/shard_map/dot_general | solution.py:50
  99.3 0.0 reduce-scatter.6.cloned.1.call-start
  99.6 4.8 %collective-permute-start.3 = (bf16[8,3072]{1,0:T(8,128)(2,1)S(1)}, bf16[8,3072]{1,0:T(8,128)(2,1)S(1)}, u32[]{:S(2)}, u32[]{:S(2)}) collective-permute-start(bf16[8,3072]{1,0:T(8,128)(2,1)S(1)} %collective-permute-done.1), channel_id=1, source_target_pairs={{0,28},{4,0},{8,4},{12,8},{16,12},{20,16},{24,20},{28,24},{1,29},{... | collective-permute-start | bytes 147464 | tf_op jit(solution)/shard_map/ppermute | solution.py:21
  104.4 1.7 collective-permute-done.3
  106.1 5.0 %collective-permute-start.5 = (bf16[8,3072]{1,0:T(8,128)(2,1)S(1)}, bf16[8,3072]{1,0:T(8,128)(2,1)S(1)}, u32[]{:S(2)}, u32[]{:S(2)}) collective-permute-start(bf16[8,3072]{1,0:T(8,128)(2,1)S(1)} %collective-permute-done.3), channel_id=1, source_target_pairs={{0,28},{4,0},{8,4},{12,8},{16,12},{20,16},{24,20},{28,24},{1,29},{... | collective-permute-start | bytes 147464 | tf_op jit(solution)/shard_map/ppermute | solution.py:21
  111.2 6.8 %collective-permute-done.4 = bf16[8,3072]{1,0:T(8,128)(2,1)S(1)} collective-permute-done((bf16[8,3072]{1,0:T(8,128)(2,1)S(1)}, bf16[8,3072]{1,0:T(8,128)(2,1)S(1)}, u32[]{:S(2)}, u32[]{:S(2)}) %collective-permute-start.4) | collective-permute-done | bytes 49184 | tf_op jit(solution)/shard_map/ppermute | solution.py:16
  118.0 6.7 %collective-permute-done.6 = bf16[8,3072]{1,0:T(8,128)(2,1)S(1)} collective-permute-done((bf16[8,3072]{1,0:T(8,128)(2,1)S(1)}, bf16[8,3072]{1,0:T(8,128)(2,1)S(1)}, u32[]{:S(2)}, u32[]{:S(2)}) %collective-permute-start.6) | collective-permute-done | bytes 49184 | tf_op jit(solution)/shard_map/ppermute | solution.py:16
  124.7 10.6 %fusion.6 = f32[64,3072]{1,0:T(8,128)} fusion(bf16[64,3072]{1,0:T(8,128)(2,1)S(1)} %constant_dynamic-update-slice_fusion, bf16[3072,3072]{1,0:T(8,128)(2,1)} %param.8), kind=kOutput, calls=%fused_computation.20 | convolution fusion | flops 1207959552 | bytes 20054016 | tf_op jit(solution)/shard_map/dot_general | solution.py:35
  135.4 0.0 reduce-scatter.14.cloned.1.call-start
  135.4 0.0 reduce-scatter.10.cloned.1.call-done
  135.5 0.0 reduce-scatter.12.cloned.1.call-done
  135.5 1.1 multiply_convert_fusion
  136.6 6.7 %all_gather.18 = bf16[64,3072]{1,0:T(8,128)(2,1)S(1)} all-gather(bf16[16,3072]{1,0:T(8,128)(2,1)S(1)} %get-tuple-element.9), channel_id=1, replica_groups=mesh['row'=8,'col'=4] {'col'}, dimensions={0}, use_global_device_ids=true | all-gather | bytes 491520 | tf_op jit(solution)/shard_map/all_gather | solution.py:63
  143.3 13.2 %fusion.10 = f32[64,3072]{1,0:T(8,128)} fusion(bf16[64,3072]{1,0:T(8,128)(2,1)S(1)} %all_gather.18, bf16[3072,3072]{1,0:T(8,128)(2,1)} %param.8), kind=kOutput, calls=%fused_computation.24 | convolution fusion | flops 1207959552 | bytes 20054016 | tf_op jit(solution)/shard_map/dot_general | solution.py:73
  156.5 0.0 reduce-scatter.8.cloned.1.call-start
  156.5 0.0 reduce-scatter.6.cloned.1.call-done
  156.6 1.0 multiply_convert_fusion.1
  157.5 6.6 %all_gather.15 = bf16[64,3072]{1,0:T(8,128)(2,1)S(1)} all-gather(bf16[16,3072]{1,0:T(8,128)(2,1)S(1)} %multiply_convert_fusion.1), channel_id=1, replica_groups=mesh['row'=8,'col'=4] {'col'}, dimensions={0}, use_global_device_ids=true | all-gather | bytes 491520 | tf_op jit(solution)/shard_map/all_gather | solution.py:38
  164.1 10.8 %fusion.7 = f32[64,3072]{1,0:T(8,128)} fusion(bf16[64,3072]{1,0:T(8,128)(2,1)S(1)} %all_gather.15, bf16[3072,3072]{1,0:T(8,128)(2,1)} %param.9), kind=kOutput, calls=%fused_computation.21 | convolution fusion | flops 1207959552 | bytes 20054016 | tf_op jit(solution)/shard_map/dot_general | solution.py:41
  174.9 9.5 %convert_bitcast_fusion = bf16[3072,3072]{0,1:T(8,128)(2,1)} fusion(bf16[64,3072]{1,0:T(8,128)(2,1)S(1)} %all_gather.18, bf16[64,3072]{1,0:T(8,128)(2,1)S(1)} %all_gather.17), kind=kOutput, calls=%fused_computation | convolution fusion | flops 1217396736 | bytes 19660800 | tf_op jit(solution)/shard_map/dot_general | solution.py:68
  184.4 24.6 %copy.9 = bf16[3072,3072]{1,0:T(8,128)(2,1)} copy(bf16[3072,3072]{0,1:T(8,128)(2,1)} %convert_bitcast_fusion) | data formatting | bytes 37748736
  209.0 6.8 %all_gather.19 = bf16[64,3072]{1,0:T(8,128)(2,1)S(1)} all-gather(bf16[16,3072]{1,0:T(8,128)(2,1)S(1)} %get-tuple-element.8), channel_id=1, replica_groups=mesh['row'=8,'col'=4] {'col'}, dimensions={0}, use_global_device_ids=true | all-gather | bytes 491520 | tf_op jit(solution)/shard_map/all_gather | solution.py:62
  215.8 9.5 %convolution_convert_fusion = bf16[3072,3072]{1,0:T(8,128)(2,1)} fusion(bf16[64,3072]{1,0:T(8,128)(2,1)S(1)} %all_gather.19, bf16[64,3072]{1,0:T(8,128)(2,1)S(1)} %all_gather.16), kind=kOutput, calls=%fused_computation.1 | convolution fusion | flops 1217396736 | bytes 19660800 | tf_op jit(solution)/shard_map/dot_general | solution.py:65
  225.3 1.5 convert_element_type.27
  226.8 61.2 %reduce-scatter.8.cloned.1.call-done = f32[8,3072]{1,0:T(8,128)} async-done(((f32[64,3072]{1,0:T(8,128)}), f32[8,3072]{1,0:T(8,128)}) %reduce-scatter.8.cloned.1.call-update) | async-done | bytes 98320 | tf_op jit(solution)/shard_map/reduce_scatter | solution.py:40
  288.1 1.5 convert_element_type.25
  (27 shorter events, 0.2 us)
Async XLA Ops:
  7.2 46.2 %copy-start.1 = (bf16[8,3072]{1,0:T(8,128)(2,1)S(1)}, bf16[8,3072]{1,0:T(8,128)(2,1)}, u32[]{:S(2)}) copy-start(bf16[8,3072]{1,0:T(8,128)(2,1)} %param.5) | copy-start | bytes 147460
  7.2 50.6 %copy-start = (bf16[8,3072]{1,0:T(8,128)(2,1)S(1)}, bf16[8,3072]{1,0:T(8,128)(2,1)}, u32[]{:S(2)}) copy-start(bf16[8,3072]{1,0:T(8,128)(2,1)} %param.6) | copy-start | bytes 147460
  7.2 128.3 %reduce-scatter.10.cloned.1.call-start = ((), (), s32[]{:S(2)}) async-start(), calls=%async_computation.7 | async-start | bytes 983040 | tf_op jit(solution)/shard_map/reduce_scatter | solution.py:56
  53.3 82.2 %reduce-scatter.12.cloned.1.call-start = ((), (), s32[]{:S(2)}) async-start(), calls=%async_computation.8 | async-start | bytes 983040 | tf_op jit(solution)/shard_map/reduce_scatter | solution.py:55
  53.4 46.2 %collective-permute-start.1 = (bf16[8,3072]{1,0:T(8,128)(2,1)S(1)}, bf16[8,3072]{1,0:T(8,128)(2,1)S(1)}, u32[]{:S(2)}, u32[]{:S(2)}) collective-permute-start(bf16[8,3072]{1,0:T(8,128)(2,1)S(1)} %copy-done.1), channel_id=1, source_target_pairs={{0,28},{4,0},{8,4},{12,8},{16,12},{20,16},{24,20},{28,24},{1,29},{... | collective-permute-start | bytes 147464 | tf_op jit(solution)/shard_map/ppermute | solution.py:21
  57.7 46.6 %collective-permute-start = (bf16[8,3072]{1,0:T(8,128)(2,1)S(1)}, bf16[8,3072]{1,0:T(8,128)(2,1)S(1)}, u32[]{:S(2)}, u32[]{:S(2)}) collective-permute-start(bf16[8,3072]{1,0:T(8,128)(2,1)S(1)} %copy-done.1), channel_id=1, source_target_pairs={{0,4},{4,8},{8,12},{12,16},{16,20},{20,24},{24,28},{28,0},{1,5},{5... | collective-permute-start | bytes 147464 | tf_op jit(solution)/shard_map/ppermute | solution.py:16
  99.3 57.2 %reduce-scatter.6.cloned.1.call-start = ((), (), s32[]{:S(2)}) async-start(), calls=%async_computation.5 | async-start | bytes 983040 | tf_op jit(solution)/shard_map/reduce_scatter | solution.py:36
  99.6 6.5 %collective-permute-start.3 = (bf16[8,3072]{1,0:T(8,128)(2,1)S(1)}, bf16[8,3072]{1,0:T(8,128)(2,1)S(1)}, u32[]{:S(2)}, u32[]{:S(2)}) collective-permute-start(bf16[8,3072]{1,0:T(8,128)(2,1)S(1)} %collective-permute-done.1), channel_id=1, source_target_pairs={{0,28},{4,0},{8,4},{12,8},{16,12},{20,16},{24,20},{28,24},{1,29},{... | collective-permute-start | bytes 147464 | tf_op jit(solution)/shard_map/ppermute | solution.py:21
  104.4 6.8 %collective-permute-start.2 = (bf16[8,3072]{1,0:T(8,128)(2,1)S(1)}, bf16[8,3072]{1,0:T(8,128)(2,1)S(1)}, u32[]{:S(2)}, u32[]{:S(2)}) collective-permute-start(bf16[8,3072]{1,0:T(8,128)(2,1)S(1)} %collective-permute-done), channel_id=1, source_target_pairs={{0,4},{4,8},{8,12},{12,16},{16,20},{20,24},{24,28},{28,0},{1,5},{5... | collective-permute-start | bytes 147464 | tf_op jit(solution)/shard_map/ppermute | solution.py:16
  106.1 11.8 %collective-permute-start.5 = (bf16[8,3072]{1,0:T(8,128)(2,1)S(1)}, bf16[8,3072]{1,0:T(8,128)(2,1)S(1)}, u32[]{:S(2)}, u32[]{:S(2)}) collective-permute-start(bf16[8,3072]{1,0:T(8,128)(2,1)S(1)} %collective-permute-done.3), channel_id=1, source_target_pairs={{0,28},{4,0},{8,4},{12,8},{16,12},{20,16},{24,20},{28,24},{1,29},{... | collective-permute-start | bytes 147464 | tf_op jit(solution)/shard_map/ppermute | solution.py:21
  111.2 6.8 %collective-permute-start.4 = (bf16[8,3072]{1,0:T(8,128)(2,1)S(1)}, bf16[8,3072]{1,0:T(8,128)(2,1)S(1)}, u32[]{:S(2)}, u32[]{:S(2)}) collective-permute-start(bf16[8,3072]{1,0:T(8,128)(2,1)S(1)} %collective-permute-done.2), channel_id=1, source_target_pairs={{0,4},{4,8},{8,12},{12,16},{16,20},{20,24},{24,28},{28,0},{1,5},{5... | collective-permute-start | bytes 147464 | tf_op jit(solution)/shard_map/ppermute | solution.py:16
  117.9 6.8 %collective-permute-start.6 = (bf16[8,3072]{1,0:T(8,128)(2,1)S(1)}, bf16[8,3072]{1,0:T(8,128)(2,1)S(1)}, u32[]{:S(2)}, u32[]{:S(2)}) collective-permute-start(bf16[8,3072]{1,0:T(8,128)(2,1)S(1)} %collective-permute-done.4), channel_id=1, source_target_pairs={{0,4},{4,8},{8,12},{12,16},{16,20},{20,24},{24,28},{28,0},{1,5},{5... | collective-permute-start | bytes 147464 | tf_op jit(solution)/shard_map/ppermute | solution.py:16
  135.4 89.9 %reduce-scatter.14.cloned.1.call-start = ((), (), s32[]{:S(2)}) async-start(), calls=%async_computation.9 | async-start | bytes 884736 | tf_op jit(solution)/shard_map/reduce_scatter | solution.py:72
  156.5 131.6 %reduce-scatter.8.cloned.1.call-start = ((), (), s32[]{:S(2)}) async-start(), calls=%async_computation.6 | async-start | bytes 884736 | tf_op jit(solution)/shard_map/reduce_scatter | solution.py:40
Sparse Core Ops, SparseCore 0:
  53.4 24.2 reduce-scatter.9
  99.5 24.6 reduce-scatter.11
  135.5 20.5 reduce-scatter.5
  159.2 63.2 reduce-scatter.13
  225.7 62.3 reduce-scatter.7
